TPU v7x, 32 devices: a whole 2x2x4 slice. The times are simulated.
32 devices in a mesh: face: 4 (over x, core), sub: 8 (over z, y).
Axes of the slice: x: 2, y: 2, z: 4, core: 2. Of those that a mesh axis runs over, the one named last changes fastest.
Arguments:
- grid_latent: bfloat16 [16384, 512], P(('face', 'sub')), may hold values from -6 to 6
- mesh_latent: bfloat16 [4096, 512], P(('face', 'sub')), may hold values from -6 to 6
- edge_latent: bfloat16 [32768, 512], P(('face', 'sub')), may hold values from -6 to 6
- mesh_cotangent: bfloat16 [4096, 512], P(('face', 'sub')), may hold values from -6 to 6
- edge_cotangent: bfloat16 [32768, 512], P(('face', 'sub')), may hold values from -6 to 6
- grid_send: int32 [32, 4, 256], P(('face', 'sub')), may hold values from 0 to 511
- grid_slot: int32 [32768], P(('face', 'sub')), may hold values from 0 to 1535, as said below
- grid_target: int32 [32768], P(('face', 'sub')), may hold values from 0 to 127
- mesh_halo: int32 [32, 4, 64], P(('face', 'sub')), may hold values from 0 to 127
- mesh_send: int32 [32, 32, 4], P(('face', 'sub')), may hold values from 0 to 127
- mesh_slot: int32 [32768], P(('face', 'sub')), may hold values from 0 to 511, as said below
- mesh_target: int32 [32768], P(('face', 'sub')), may hold values from 0 to 127
- weights: bfloat16 [10, 512, 512], replicated, may hold values from -0.25 to 0.25
Outputs:
- mesh_update: bfloat16 [4096, 512], P(('face', 'sub'))
- grid_grad: bfloat16 [16384, 512], P(('face', 'sub'))
- mesh_grad: bfloat16 [4096, 512], P(('face', 'sub'))
- edge_grad: bfloat16 [32768, 512], P(('face', 'sub'))
- weight_grads: bfloat16 [10, 512, 512], replicated
Inputs may be any that keep to these rules, and one draw needn't show every extreme that they name: grid_slot[e] names the edge device's own 512 grid rows or, above them, the 256 rows listed by each of its four neighbours in direction order. grid_target[e] is local to the edge's device. grid_send[q, k] lists local rows of device q for the device d with nb(d, k) = q; a row may appear in several slots. mesh_slot[e] names the own 128 mesh rows, then the 64 rows listed by each of the four neighbours, then 4 far rows from each device, source major. mesh_target[e] is local to the edge's device. mesh_halo[q, k] lists local rows of device q for its neighbour in direction k. mesh_send[q, d] lists local rows of device q for far edges of device d.
All inputs are finite; a program needn't handle non-finite values.
Results may differ from a plain program's by a relative error of at most 0.016.
Values may be sent and summed in bfloat16 or wider, within the bound.
A program may use at most 128 MiB of HBM per device.

v0:
```python
import jax
import jax.numpy as jnp
from jax import lax
from jax.sharding import PartitionSpec as P

norm_eps = 1e-05


def shifted(value, axis, steps):
    count = lax.axis_size(axis)
    pairs = [(source, (source + steps) % count) for source in range(count)]
    return lax.ppermute(value, axis, pairs)


def layer_norm(values):
    centre = values - jnp.mean(values, axis=-1, keepdims=True)
    spread = jnp.mean(centre * centre, axis=-1, keepdims=True)
    return centre * lax.rsqrt(spread + norm_eps)


def layer_norm_back(values, upstream):
    centre = values - jnp.mean(values, axis=-1, keepdims=True)
    inverse = lax.rsqrt(jnp.mean(centre * centre, axis=-1, keepdims=True) + norm_eps)
    normed = centre * inverse
    return inverse * (
        upstream
        - jnp.mean(upstream, axis=-1, keepdims=True)
        - normed * jnp.mean(upstream * normed, axis=-1, keepdims=True)
    )


def swish_slope(values):
    sigmoid_values = jax.nn.sigmoid(values)
    return sigmoid_values * (1.0 + values * (1.0 - sigmoid_values))


def product(former, latter):
    return jnp.dot(former, latter, preferred_element_type=jnp.float32)


def outer_sum(former, latter):
    return lax.dot_general(
        former, latter, (((0,), (0,)), ((), ())), preferred_element_type=jnp.float32
    )


def back_product(former, latter):
    return lax.dot_general(
        former, latter, (((1,), (1,)), ((), ())), preferred_element_type=jnp.float32
    )


def select_columns(ids, count):
    columns = lax.broadcasted_iota(jnp.int32, (ids.shape[0], count), 1)
    return (ids[:, None] == columns).astype(jnp.bfloat16)


def select_pair(ids, others, count, other_count):
    columns = lax.broadcasted_iota(jnp.int32, (ids.shape[0], count + other_count), 1)
    hit = (ids[:, None] == columns) | ((others + count)[:, None] == columns)
    return hit.astype(jnp.bfloat16)


def stack_grads(terms):
    return jnp.stack([term.astype(jnp.bfloat16) for term in terms])


def grid_neighbours(outgoing):
    from_sub = [shifted(outgoing[block], "sub", offset) for block, offset in ((0, 1), (1, -1))]
    from_face = [shifted(outgoing[block], "face", offset) for block, offset in ((2, 1), (3, -1))]
    return jnp.concatenate(from_sub + from_face, axis=0)


def grid_returns(partials):
    to_sub = [shifted(partials[block], "sub", offset) for block, offset in ((0, -1), (1, 1))]
    to_face = [shifted(partials[block], "face", offset) for block, offset in ((2, -1), (3, 1))]
    return jnp.concatenate(to_sub + to_face, axis=0)


def mesh_neighbours(outgoing):
    from_sub = [shifted(outgoing[block], "sub", offset) for block, offset in ((0, 1), (1, -1))]
    from_face = [shifted(outgoing[block], "face", offset) for block, offset in ((2, 1), (3, -1))]
    return jnp.concatenate(from_sub + from_face, axis=0)


def mesh_returns(partials):
    to_sub = [shifted(partials[block], "sub", offset) for block, offset in ((0, -1), (1, 1))]
    to_face = [shifted(partials[block], "face", offset) for block, offset in ((2, -1), (3, 1))]
    return jnp.concatenate(to_sub + to_face, axis=0)


def move_mesh(outgoing):
    return lax.all_to_all(outgoing, ("face", "sub"), split_axis=0, concat_axis=0, tiled=True)


def return_mesh(outgoing):
    return lax.all_to_all(outgoing, ("face", "sub"), split_axis=0, concat_axis=0, tiled=True)


def on_device(
    grid_latent,
    mesh_latent,
    edge_latent,
    mesh_cotangent,
    edge_cotangent,
    grid_send,
    grid_slot,
    grid_target,
    mesh_halo,
    mesh_send,
    mesh_slot,
    mesh_target,
    weights,
):
    peer_count = lax.axis_size("face") * lax.axis_size("sub")
    latent = weights.shape[1]
    mesh_rows = mesh_latent.shape[0]
    grid_rows = grid_latent.shape[0]
    grid_table = grid_send[0].reshape(-1)
    halo_table = mesh_halo[0].reshape(-1)
    far_table = mesh_send[0].reshape(-1)
    halo_count = halo_table.shape[0]
    slot_count = mesh_rows + halo_count + far_table.shape[0]
    grid_slot_count = grid_rows + grid_table.shape[0]
    pick_grid = select_columns(grid_table, grid_rows)
    pick_halo_far = select_columns(jnp.concatenate([halo_table, far_table]), mesh_rows)
    grid_pair = select_pair(grid_slot, grid_target, grid_slot_count, mesh_rows)
    mesh_pair = select_pair(mesh_slot, mesh_target, slot_count, mesh_rows)
    grid_onehot = select_columns(grid_target, mesh_rows)
    mesh_onehot = select_columns(mesh_target, mesh_rows)
    encode_scale = 1.0 / (grid_slot.shape[0] * peer_count) ** 0.5
    process_scale = 1.0 / (mesh_slot.shape[0] * peer_count) ** 0.5
    update_scale = 1.0 / (mesh_rows * peer_count) ** 0.5
    grid_project = product(grid_latent, weights[0]).astype(jnp.bfloat16)
    grid_outgoing = product(pick_grid, grid_project).astype(jnp.bfloat16).reshape(4, -1, latent)
    encode_receive = product(mesh_latent, weights[1]).astype(jnp.bfloat16)
    grid_source = jnp.concatenate(
        [grid_project, grid_neighbours(grid_outgoing), encode_receive], axis=0
    )
    encoder_pre = product(grid_pair, grid_source)
    encoder_hidden = jax.nn.silu(encoder_pre).astype(jnp.bfloat16)
    encoder_linear = product(encoder_hidden, weights[2])
    encoder_message = layer_norm(encoder_linear).astype(jnp.bfloat16)
    encoder_total = outer_sum(grid_onehot, encoder_message)
    mesh_middle = (mesh_latent.astype(jnp.float32) + encoder_total).astype(jnp.bfloat16)
    sender_rows = product(mesh_middle, weights[4]).astype(jnp.bfloat16)
    outgoing = product(pick_halo_far, sender_rows).astype(jnp.bfloat16)
    halo_outgoing = outgoing[:halo_count].reshape(4, -1, latent)
    far_outgoing = outgoing[halo_count:].reshape(peer_count, -1, latent)
    far_incoming = move_mesh(far_outgoing).reshape(-1, latent)
    process_receive = product(mesh_middle, weights[5]).astype(jnp.bfloat16)
    mesh_source = jnp.concatenate(
        [sender_rows, mesh_neighbours(halo_outgoing), far_incoming, process_receive], axis=0
    )
    process_pre = product(edge_latent, weights[3]) + product(mesh_pair, mesh_source)
    process_hidden = jax.nn.silu(process_pre).astype(jnp.bfloat16)
    process_linear = product(process_hidden, weights[6])
    edge_update = layer_norm(process_linear).astype(jnp.bfloat16)
    process_round = outer_sum(mesh_onehot, edge_update).astype(jnp.bfloat16)
    update_pre = product(mesh_middle, weights[7]) + product(process_round, weights[8])
    update_hidden = jax.nn.silu(update_pre).astype(jnp.bfloat16)
    update_linear = product(update_hidden, weights[9])
    mesh_update = (mesh_middle.astype(jnp.float32) + layer_norm(update_linear)).astype(jnp.bfloat16)
    outer_cot = mesh_cotangent.astype(jnp.float32)
    cot_linear = layer_norm_back(update_linear, outer_cot).astype(jnp.bfloat16)
    grad_update_output = outer_sum(update_hidden, cot_linear)
    cot_update = (back_product(cot_linear, weights[9]) * swish_slope(update_pre)).astype(
        jnp.bfloat16
    )
    grad_update_self = outer_sum(mesh_middle, cot_update)
    grad_update_message = outer_sum(process_round, cot_update)
    cot_total = back_product(cot_update, weights[8]).astype(jnp.bfloat16)
    edge_cot = edge_cotangent.astype(jnp.float32)
    cot_edge = product(mesh_onehot, cot_total) + edge_cot
    cot_plinear = layer_norm_back(process_linear, cot_edge).astype(jnp.bfloat16)
    grad_process_output = outer_sum(process_hidden, cot_plinear)
    cot_process = back_product(cot_plinear, weights[6]) * swish_slope(process_pre)
    cot_round = cot_process.astype(jnp.bfloat16)
    grad_process_edge = outer_sum(edge_latent, cot_round)
    edge_grad = (edge_cot + back_product(cot_round, weights[3])).astype(jnp.bfloat16)
    cot_slot = outer_sum(mesh_pair, cot_round)
    cot_receive = cot_slot[slot_count:].astype(jnp.bfloat16)
    grad_process_receiver = outer_sum(mesh_middle, cot_receive)
    halo_partials = (
        cot_slot[mesh_rows : mesh_rows + halo_count].astype(jnp.bfloat16).reshape(4, -1, latent)
    )
    far_partials = (
        cot_slot[mesh_rows + halo_count : slot_count]
        .astype(jnp.bfloat16)
        .reshape(peer_count, -1, latent)
    )
    far_returned = return_mesh(far_partials).reshape(-1, latent)
    returned = jnp.concatenate([mesh_returns(halo_partials), far_returned], axis=0)
    sender_total = cot_slot[:mesh_rows] + outer_sum(pick_halo_far, returned)
    cot_sender = sender_total.astype(jnp.bfloat16)
    grad_process_sender = outer_sum(mesh_middle, cot_sender)
    cot_middle = (
        outer_cot
        + back_product(cot_update, weights[7])
        + back_product(cot_receive, weights[5])
        + back_product(cot_sender, weights[4])
    )
    process_grads = stack_grads(
        [
            grad_process_edge,
            grad_process_sender,
            grad_process_receiver,
            grad_process_output,
            grad_update_self,
            grad_update_message,
            grad_update_output,
        ]
    )
    process_grads = lax.psum(process_grads, ("face", "sub"))
    cot_message = product(grid_onehot, cot_middle.astype(jnp.bfloat16))
    cot_elinear = layer_norm_back(encoder_linear, cot_message).astype(jnp.bfloat16)
    grad_encode_output = outer_sum(encoder_hidden, cot_elinear)
    cot_encoder = back_product(cot_elinear, weights[2]) * swish_slope(encoder_pre)
    cot_gslot = outer_sum(grid_pair, cot_encoder.astype(jnp.bfloat16))
    cot_mesh_receive = cot_gslot[grid_slot_count:].astype(jnp.bfloat16)
    grad_encode_receiver = outer_sum(mesh_latent, cot_mesh_receive)
    mesh_grad = (cot_middle + back_product(cot_mesh_receive, weights[1])).astype(jnp.bfloat16)
    grid_partials = cot_gslot[grid_rows:grid_slot_count].astype(jnp.bfloat16).reshape(4, -1, latent)
    grid_returned = grid_returns(grid_partials)
    cot_grid = (cot_gslot[:grid_rows] + outer_sum(pick_grid, grid_returned)).astype(jnp.bfloat16)
    grad_encode_sender = outer_sum(grid_latent, cot_grid)
    grid_grad = back_product(cot_grid, weights[0]).astype(jnp.bfloat16)
    encode_grads = stack_grads([grad_encode_sender, grad_encode_receiver, grad_encode_output])
    encode_grads, process_grads = lax.optimization_barrier((encode_grads, process_grads))
    encode_grads = lax.psum(encode_grads, ("face", "sub"))
    summed = jnp.concatenate([encode_grads, process_grads], axis=0).astype(jnp.float32)
    scale_column = jnp.array(
        [encode_scale] * 3 + [process_scale] * 4 + [update_scale] * 3, jnp.float32
    )
    weight_grads = (summed * scale_column[:, None, None]).astype(jnp.bfloat16)
    return (mesh_update, grid_grad, mesh_grad, edge_grad, weight_grads)


def solution(mesh):
    return jax.shard_map(
        on_device,
        mesh=mesh,
        in_specs=(
            P(("face", "sub"), None),
            P(("face", "sub"), None),
            P(("face", "sub"), None),
            P(("face", "sub"), None),
            P(("face", "sub"), None),
            P(("face", "sub"), None, None),
            P(("face", "sub")),
            P(("face", "sub")),
            P(("face", "sub"), None, None),
            P(("face", "sub"), None, None),
            P(("face", "sub")),
            P(("face", "sub")),
            P(),
        ),
        out_specs=(
            P(("face", "sub"), None),
            P(("face", "sub"), None),
            P(("face", "sub"), None),
            P(("face", "sub"), None),
            P(),
        ),
        check_vma=False,
    )
```

profile of v0, /device:TPU:0, one launch (start us, length us, event | category | flops | bytes accessed | tf_op | source)
XLA Modules:
  0.0 431.3 jit_solution(9846801557097275770)
XLA Ops:
  8.0 2.5 constant_dynamic-update-slice_fusion.4
  12.2 2.5 collective-permute-start.3
  14.7 4.6 %collective-permute-start.1 = (bf16[256,512]{1,0:T(8,128)(2,1)}, bf16[256,512]{1,0:T(8,128)(2,1)S(1)}, u32[]{:S(2)}, u32[]{:S(2)}) collective-permute-start(bf16[256,512]{1,0:T(8,128)(2,1)} %get-tuple-element.31), channel_id=1, source_target_pairs={{0,7},{1,0},{2,1},{3,2},{4,3},{5,4},{6,5},{7,6},{8,15},{9,8},{10,9... | collective-permute-start | bytes 786440 | tf_op jit(solution)/shard_map/ppermute | solution.py:12
  19.2 3.1 fusion.81
  24.0 6.8 %collective-permute-done = bf16[256,512]{1,0:T(8,128)(2,1)S(1)} collective-permute-done((bf16[256,512]{1,0:T(8,128)(2,1)}, bf16[256,512]{1,0:T(8,128)(2,1)S(1)}, u32[]{:S(2)}, u32[]{:S(2)}) %collective-permute-start) | collective-permute-done | bytes 262176 | tf_op jit(solution)/shard_map/ppermute | solution.py:12
  33.7 1.9 fusion.50
  35.6 3.6 fusion.3
  39.2 2.3 fusion.146
  42.6 1.9 constant_dynamic-update-slice_fusion.10
  48.5 1.6 reshape.127
  50.1 5.0 %all-to-all-start = ((bf16[32,4,512]{2,1,0:T(4,128)(2,1)}), bf16[32,4,512]{2,1,0:T(4,128)(2,1)}, u32[]{:S(2)}, u32[]{:S(2)}) async-start(bf16[32,4,512]{2,1,0:T(4,128)(2,1)} %reshape.127), calls=%async_computation | async-start | bytes 262144 | tf_op jit(solution)/shard_map/all_to_all | solution.py:93
  55.1 1.5 collective-permute-start.7
  56.6 4.3 collective-permute-start.5
  60.9 1.5 constant_dynamic-update-slice_fusion.9
  65.3 1.6 reshape.128
  66.9 1.6 constant_dynamic-update-slice_fusion.5
  68.4 1.9 fusion.49
  70.4 3.0 fusion.17
  73.3 2.3 fusion.147
  78.5 1.5 fusion.148
  82.4 2.1 convolution_add_fusion.4
  84.5 4.3 %fusion.141 = (f32[1024]{0:T(1024)S(1)}, f32[1024]{0:T(1024)S(1)}, f32[1024,512]{0,1:T(8,128)}) fusion(f32[1024]{0:T(1024)S(1)} %add_rsqrt_fusion, f32[1024,512]{0,1:T(8,128)} %copy-done.2, f32[1024]{0:T(1024)S(1)} %broadcast_multiply_fusion.4, bf16[1024,512]{0,1:T(8,128)(2,1)} %copy.32, bf16[128,512]{1,0:T(8,128)(2,1)S(1)} %fusion.46, ...), kind=kOutput, calls=%fused_computation.216 | convolution fusion | flops 205191168 | bytes 5918720 | tf_op jit(solution)/shard_map/dot_general | solution.py:38
  88.9 2.9 multiply_convert_fusion.4
  91.9 2.7 multiply_convert_fusion.3
  94.6 2.6 fusion.151
  97.2 1.5 fusion.30
  98.7 5.1 %collective-permute-start.8 = (bf16[64,512]{1,0:T(8,128)(2,1)S(1)}, bf16[64,512]{1,0:T(8,128)(2,1)S(1)}, u32[]{:S(2)}, u32[]{:S(2)}) collective-permute-start(bf16[64,512]{1,0:T(8,128)(2,1)S(1)} %get-tuple-element.36), channel_id=1, source_target_pairs={{0,7},{1,0},{2,1},{3,2},{4,3},{5,4},{6,5},{7,6},{8,15},{9,8},{10,9... | collective-permute-start | bytes 196616 | tf_op jit(solution)/shard_map/ppermute | solution.py:12
  106.0 2.6 all-to-all-start.1
  108.8 1.6 collective-permute-start.10
  110.4 1.7 collective-permute-start.9
  112.1 5.6 %collective-permute-done.9 = bf16[64,512]{1,0:T(8,128)(2,1)S(1)} collective-permute-done((bf16[64,512]{1,0:T(8,128)(2,1)S(1)}, bf16[64,512]{1,0:T(8,128)(2,1)S(1)}, u32[]{:S(2)}, u32[]{:S(2)}) %collective-permute-start.9) | collective-permute-done | bytes 65568 | tf_op jit(solution)/shard_map/ppermute | solution.py:12
  120.5 1.9 fusion.140
  123.6 2.0 fusion.38
  125.7 1.6 fusion.33
  131.0 2.1 multiply_convert_fusion.2
  133.2 6.9 %fusion.152 = (bf16[1664,512]{1,0:T(8,128)(2,1)S(1)}, f32[1664,512]{1,0:T(8,128)}) fusion(f32[1024,512]{1,0:T(8,128)} %copy-done.55, bf16[1024,512]{0,1:T(8,128)(2,1)S(1)} %multiply_convert_fusion.2, bf16[10,512,512]{2,1,0:T(8,128)(2,1)} %param.26, s32[1024]{0:T(1024)S(1)} %copy-done.32, s32[1024]{0:T(1024)S(1)} %copy-done.50), kind=kOutput, calls=%fused_computation.225 | convolution fusion | flops 2292383744 | bytes 8790016 | tf_op jit(solution)/shard_map/dot_general | solution.py:42
  140.2 1.4 collective-permute-start.12
  141.6 1.7 collective-permute-start.14
  145.2 8.8 %collective-permute-done.12 = bf16[256,512]{1,0:T(8,128)(2,1)S(1)} collective-permute-done((bf16[256,512]{1,0:T(8,128)(2,1)S(1)}, bf16[256,512]{1,0:T(8,128)(2,1)S(1)}, u32[]{:S(2)}, u32[]{:S(2)}) %collective-permute-start.12) | collective-permute-done | bytes 262176 | tf_op jit(solution)/shard_map/ppermute | solution.py:12
  154.0 5.5 %collective-permute-done.13 = bf16[256,512]{1,0:T(8,128)(2,1)S(1)} collective-permute-done((bf16[256,512]{1,0:T(8,128)(2,1)S(1)}, bf16[256,512]{1,0:T(8,128)(2,1)S(1)}, u32[]{:S(2)}, u32[]{:S(2)}) %collective-permute-start.13) | collective-permute-done | bytes 262176 | tf_op jit(solution)/shard_map/ppermute | solution.py:12
  159.5 2.3 fusion.28
  163.6 109.1 %all-reduce.3.cloned.1.call-done = bf16[7,512,512]{1,2,0:T(8,128)(2,1)} async-done(((bf16[7,512,512]{1,2,0:T(8,128)(2,1)}), bf16[7,512,512]{1,2,0:T(8,128)(2,1)}) %all-reduce.3.cloned.1.call-update) | async-done | bytes 3670032 | tf_op jit(solution)/shard_map/psum | solution.py:214
  272.7 2.1 fusion.10
  276.1 2.1 fusion.48
  278.2 2.3 convolution_convert_fusion.1
  280.5 129.4 %all-reduce.5.cloned.1.call-done = bf16[3,512,512]{1,2,0:T(8,128)(2,1)} async-done(((bf16[3,512,512]{1,2,0:T(8,128)(2,1)}), bf16[3,512,512]{1,2,0:T(8,128)(2,1)}) %all-reduce.5.cloned.1.call-update) | async-done | bytes 1572880 | tf_op jit(solution)/shard_map/psum | solution.py:230
  409.9 6.5 %multiply_convert_fusion = bf16[10,512,512]{1,2,0:T(8,128)(2,1)} fusion(bf16[7,512,512]{1,2,0:T(8,128)(2,1)} %all-reduce.3.cloned.1.call-done, bf16[3,512,512]{1,2,0:T(8,128)(2,1)} %all-reduce.5.cloned.1.call-done, f32[10]{0:T(128)S(1)} %copy-done.45), kind=kLoop, calls=%fused_computation | loop fusion | flops 10485760 | bytes 10485800 | tf_op jit(solution)/shard_map/convert_element_type | solution.py:235
  416.4 8.0 %copy.42 = bf16[10,512,512]{2,1,0:T(8,128)(2,1)} copy(bf16[10,512,512]{1,2,0:T(8,128)(2,1)} %multiply_convert_fusion) | data formatting | bytes 10485760
  (201 shorter events, 35.1 us)
Async XLA Ops:
  7.2 12.1 %copy-start = (bf16[1024,512]{1,0:T(8,128)(2,1)S(1)}, bf16[1024,512]{1,0:T(8,128)(2,1)}, u32[]{:S(2)}) copy-start(bf16[1024,512]{1,0:T(8,128)(2,1)} %param.16) | copy-start | bytes 3145732
  10.4 8.8 %copy-start.25 = (s32[1024]{0:T(1024)S(1)}, s32[1024]{0:T(1024)}, u32[]{:S(2)}) copy-start(s32[1024]{0:T(1024)} %param.21) | copy-start | bytes 12292
  12.2 10.1 %copy-start.22 = (s32[1024]{0:T(1024)S(1)}, s32[1024]{0:T(1024)}, u32[]{:S(2)}) copy-start(s32[1024]{0:T(1024)} %param.25) | copy-start | bytes 12292
  12.2 10.1 %copy-start.38 = (s32[1,4,64]{2,1,0:T(4,128)S(1)}, s32[1,4,64]{2,1,0:T(4,128)}, u32[]{:S(2)}) copy-start(s32[1,4,64]{2,1,0:T(4,128)} %param.22) | copy-start | bytes 3076
  12.2 10.2 %copy-start.37 = (s32[1,32,4]{1,2,0:T(4,128)S(1)}, s32[1,32,4]{1,2,0:T(4,128)}, u32[]{:S(2)}) copy-start(s32[1,32,4]{1,2,0:T(4,128)} %param.23) | copy-start | bytes 1540
  12.2 10.4 %copy-start.10 = (bf16[1024,512]{1,0:T(8,128)(2,1)S(1)}, bf16[1024,512]{1,0:T(8,128)(2,1)}, u32[]{:S(2)}) copy-start(bf16[1024,512]{1,0:T(8,128)(2,1)} %param.18) | copy-start | bytes 3145732
  12.2 20.8 %collective-permute-start.3 = (bf16[256,512]{1,0:T(8,128)(2,1)}, bf16[256,512]{1,0:T(8,128)(2,1)S(1)}, u32[]{:S(2)}, u32[]{:S(2)}) collective-permute-start(bf16[256,512]{1,0:T(8,128)(2,1)} %get-tuple-element.29), channel_id=1, source_target_pairs={{0,24},{8,0},{16,8},{24,16},{1,25},{9,1},{17,9},{25,17},{2,26},{10... | collective-permute-start | bytes 786440 | tf_op jit(solution)/shard_map/ppermute | solution.py:12
  14.7 17.6 %collective-permute-start.2 = (bf16[256,512]{1,0:T(8,128)(2,1)}, bf16[256,512]{1,0:T(8,128)(2,1)S(1)}, u32[]{:S(2)}, u32[]{:S(2)}) collective-permute-start(bf16[256,512]{1,0:T(8,128)(2,1)} %get-tuple-element.30), channel_id=1, source_target_pairs={{0,8},{8,16},{16,24},{24,0},{1,9},{9,17},{17,25},{25,1},{2,10},{10... | collective-permute-start | bytes 786440 | tf_op jit(solution)/shard_map/ppermute | solution.py:12
  14.7 16.9 %collective-permute-start.1 = (bf16[256,512]{1,0:T(8,128)(2,1)}, bf16[256,512]{1,0:T(8,128)(2,1)S(1)}, u32[]{:S(2)}, u32[]{:S(2)}) collective-permute-start(bf16[256,512]{1,0:T(8,128)(2,1)} %get-tuple-element.31), channel_id=1, source_target_pairs={{0,7},{1,0},{2,1},{3,2},{4,3},{5,4},{6,5},{7,6},{8,15},{9,8},{10,9... | collective-permute-start | bytes 786440 | tf_op jit(solution)/shard_map/ppermute | solution.py:12
  19.2 11.6 %collective-permute-start = (bf16[256,512]{1,0:T(8,128)(2,1)}, bf16[256,512]{1,0:T(8,128)(2,1)S(1)}, u32[]{:S(2)}, u32[]{:S(2)}) collective-permute-start(bf16[256,512]{1,0:T(8,128)(2,1)} %get-tuple-element.32), channel_id=1, source_target_pairs={{0,1},{1,2},{2,3},{3,4},{4,5},{5,6},{6,7},{7,0},{8,9},{9,10},{10,1... | collective-permute-start | bytes 786440 | tf_op jit(solution)/shard_map/ppermute | solution.py:12
  19.2 16.4 %copy-start.31 = (s32[1024]{0:T(1024)}, s32[1024]{0:T(1024)S(1)}, u32[]{:S(2)}) copy-start(s32[1024]{0:T(1024)S(1)} %broadcast_add_fusion.1) | copy-start | bytes 12292
  22.3 48.0 %copy-start.33 = (s32[1024]{0:T(1024)}, s32[1024]{0:T(1024)S(1)}, u32[]{:S(2)}) copy-start(s32[1024]{0:T(1024)S(1)} %broadcast_add_fusion) | copy-start | bytes 12292
  22.6 21.9 %copy-start.27 = (s32[384]{0:T(512)}, s32[384]{0:T(512)S(1)}, u32[]{:S(2)}) copy-start(s32[384]{0:T(512)S(1)} %pad_add_fusion) | copy-start | bytes 4612
  22.6 11.0 %copy-start.16 = (bf16[128,512]{1,0:T(8,128)(2,1)S(1)}, bf16[128,512]{1,0:T(8,128)(2,1)}, u32[]{:S(2)}) copy-start(bf16[128,512]{1,0:T(8,128)(2,1)} %param.15) | copy-start | bytes 393220
  22.7 13.0 %copy-start.49 = (s32[1024]{0:T(1024)S(1)}, s32[1024]{0:T(1024)}, u32[]{:S(2)}) copy-start(s32[1024]{0:T(1024)} %param.20) | copy-start | bytes 12292
  44.8 25.5 %copy-start.47 = (s32[1024]{0:T(1024)S(1)}, s32[1024]{0:T(1024)}, u32[]{:S(2)}) copy-start(s32[1024]{0:T(1024)} %param.24) | copy-start | bytes 12292
  45.5 15.3 %collective-permute-start.4 = (bf16[64,512]{1,0:T(8,128)(2,1)}, bf16[64,512]{1,0:T(8,128)(2,1)}, u32[]{:S(2)}, u32[]{:S(2)}) collective-permute-start(bf16[64,512]{1,0:T(8,128)(2,1)} %get-tuple-element.40), channel_id=1, source_target_pairs={{0,1},{1,2},{2,3},{3,4},{4,5},{5,6},{6,7},{7,0},{8,9},{9,10},{10,1... | collective-permute-start | bytes 196616 | tf_op jit(solution)/shard_map/ppermute | solution.py:12
  50.1 15.1 %all-to-all-start = ((bf16[32,4,512]{2,1,0:T(4,128)(2,1)}), bf16[32,4,512]{2,1,0:T(4,128)(2,1)}, u32[]{:S(2)}, u32[]{:S(2)}) async-start(bf16[32,4,512]{2,1,0:T(4,128)(2,1)} %reshape.127), calls=%async_computation | async-start | bytes 262144 | tf_op jit(solution)/shard_map/all_to_all | solution.py:93
  55.1 9.5 %collective-permute-start.7 = (bf16[64,512]{1,0:T(8,128)(2,1)}, bf16[64,512]{1,0:T(8,128)(2,1)S(1)}, u32[]{:S(2)}, u32[]{:S(2)}) collective-permute-start(bf16[64,512]{1,0:T(8,128)(2,1)} %get-tuple-element.37), channel_id=1, source_target_pairs={{0,24},{8,0},{16,8},{24,16},{1,25},{9,1},{17,9},{25,17},{2,26},{10... | collective-permute-start | bytes 196616 | tf_op jit(solution)/shard_map/ppermute | solution.py:12
  56.6 7.4 %collective-permute-start.6 = (bf16[64,512]{1,0:T(8,128)(2,1)}, bf16[64,512]{1,0:T(8,128)(2,1)S(1)}, u32[]{:S(2)}, u32[]{:S(2)}) collective-permute-start(bf16[64,512]{1,0:T(8,128)(2,1)} %get-tuple-element.38), channel_id=1, source_target_pairs={{0,8},{8,16},{16,24},{24,0},{1,9},{9,17},{17,25},{25,1},{2,10},{10... | collective-permute-start | bytes 196616 | tf_op jit(solution)/shard_map/ppermute | solution.py:12
  56.6 6.8 %collective-permute-start.5 = (bf16[64,512]{1,0:T(8,128)(2,1)}, bf16[64,512]{1,0:T(8,128)(2,1)S(1)}, u32[]{:S(2)}, u32[]{:S(2)}) collective-permute-start(bf16[64,512]{1,0:T(8,128)(2,1)} %get-tuple-element.39), channel_id=1, source_target_pairs={{0,7},{1,0},{2,1},{3,2},{4,3},{5,4},{6,5},{7,6},{8,15},{9,8},{10,9... | collective-permute-start | bytes 196616 | tf_op jit(solution)/shard_map/ppermute | solution.py:12
  77.1 5.3 %copy-start.6 = (bf16[128,512]{1,0:T(8,128)(2,1)}, bf16[128,512]{1,0:T(8,128)(2,1)S(1)}, u32[]{:S(2)}) copy-start(bf16[128,512]{1,0:T(8,128)(2,1)S(1)} %convolution_convert_fusion.17) | copy-start | bytes 393220
  80.2 4.3 %copy-start.39 = (f32[128]{0:T(128)}, f32[128]{0:T(128)S(1)}, u32[]{:S(2)}) copy-start(f32[128]{0:T(128)S(1)} %add_rsqrt_fusion.2) | copy-start | bytes 1540
  81.0 7.9 %copy-start.41 = (f32[128]{0:T(128)}, f32[128]{0:T(128)S(1)}, u32[]{:S(2)}) copy-start(f32[128]{0:T(128)S(1)} %get-tuple-element.58) | copy-start | bytes 1540
  81.0 7.9 %copy-start.43 = (f32[128]{0:T(128)}, f32[128]{0:T(128)S(1)}, u32[]{:S(2)}) copy-start(f32[128]{0:T(128)S(1)} %get-tuple-element.59) | copy-start | bytes 1540
  82.4 6.5 %copy-start.4 = (bf16[128,512]{1,0:T(8,128)(2,1)}, bf16[128,512]{1,0:T(8,128)(2,1)S(1)}, u32[]{:S(2)}) copy-start(bf16[128,512]{1,0:T(8,128)(2,1)S(1)} %fusion.46) | copy-start | bytes 393220
  97.2 8.1 %copy-start.15 = (bf16[640,512]{1,0:T(8,128)(2,1)}, bf16[640,512]{1,0:T(8,128)(2,1)S(1)}, u32[]{:S(2)}) copy-start(bf16[640,512]{1,0:T(8,128)(2,1)S(1)} %get-tuple-element.53) | copy-start | bytes 1966084
  97.2 6.7 %copy-start.13 = (f32[128,512]{1,0:T(8,128)S(1)}, f32[128,512]{1,0:T(8,128)}, u32[]{:S(2)}) copy-start(f32[128,512]{1,0:T(8,128)} %convolution_add_fusion.4) | copy-start | bytes 786436
  98.7 19.1 %copy-start.28 = (s32[384]{0:T(512)S(1)}, s32[384]{0:T(512)}, u32[]{:S(2)}) copy-start(s32[384]{0:T(512)} %copy-done.27) | copy-start | bytes 4612
  98.7 13.3 %collective-permute-start.8 = (bf16[64,512]{1,0:T(8,128)(2,1)S(1)}, bf16[64,512]{1,0:T(8,128)(2,1)S(1)}, u32[]{:S(2)}, u32[]{:S(2)}) collective-permute-start(bf16[64,512]{1,0:T(8,128)(2,1)S(1)} %get-tuple-element.36), channel_id=1, source_target_pairs={{0,7},{1,0},{2,1},{3,2},{4,3},{5,4},{6,5},{7,6},{8,15},{9,8},{10,9... | collective-permute-start | bytes 196616 | tf_op jit(solution)/shard_map/ppermute | solution.py:12
  105.2 15.2 %copy-start.26 = (s32[1024]{0:T(1024)S(1)}, s32[1024]{0:T(1024)}, u32[]{:S(2)}) copy-start(s32[1024]{0:T(1024)} %param.21) | copy-start | bytes 12292
  106.0 11.8 %all-to-all-start.1 = ((bf16[32,4,512]{2,1,0:T(4,128)(2,1)}), bf16[32,4,512]{2,1,0:T(4,128)(2,1)S(1)}, u32[]{:S(2)}, u32[]{:S(2)}) async-start(bf16[32,4,512]{2,1,0:T(4,128)(2,1)} %reshape.129), calls=%async_computation.1 | async-start | bytes 262144 | tf_op jit(solution)/shard_map/all_to_all | solution.py:97
  108.5 164.1 %all-reduce.3.cloned.1.call-start = ((), (), s32[]{:S(2)}) async-start(), calls=%async_computation.2 | async-start | bytes 7340032 | tf_op jit(solution)/shard_map/psum | solution.py:214
  108.6 9.1 %collective-permute-start.11 = (bf16[64,512]{1,0:T(8,128)(2,1)S(1)}, bf16[64,512]{1,0:T(8,128)(2,1)S(1)}, u32[]{:S(2)}, u32[]{:S(2)}) collective-permute-start(bf16[64,512]{1,0:T(8,128)(2,1)S(1)} %get-tuple-element.33), channel_id=1, source_target_pairs={{0,8},{8,16},{16,24},{24,0},{1,9},{9,17},{17,25},{25,1},{2,10},{10... | collective-permute-start | bytes 196616 | tf_op jit(solution)/shard_map/ppermute | solution.py:12
  108.8 8.9 %collective-permute-start.10 = (bf16[64,512]{1,0:T(8,128)(2,1)S(1)}, bf16[64,512]{1,0:T(8,128)(2,1)S(1)}, u32[]{:S(2)}, u32[]{:S(2)}) collective-permute-start(bf16[64,512]{1,0:T(8,128)(2,1)S(1)} %get-tuple-element.34), channel_id=1, source_target_pairs={{0,24},{8,0},{16,8},{24,16},{1,25},{9,1},{17,9},{25,17},{2,26},{10... | collective-permute-start | bytes 196616 | tf_op jit(solution)/shard_map/ppermute | solution.py:12
  110.4 7.3 %collective-permute-start.9 = (bf16[64,512]{1,0:T(8,128)(2,1)S(1)}, bf16[64,512]{1,0:T(8,128)(2,1)S(1)}, u32[]{:S(2)}, u32[]{:S(2)}) collective-permute-start(bf16[64,512]{1,0:T(8,128)(2,1)S(1)} %get-tuple-element.35), channel_id=1, source_target_pairs={{0,1},{1,2},{2,3},{3,4},{4,5},{5,6},{6,7},{7,0},{8,9},{9,10},{10,1... | collective-permute-start | bytes 196616 | tf_op jit(solution)/shard_map/ppermute | solution.py:12
  120.5 5.1 %copy-start.9 = (bf16[1024,512]{0,1:T(8,128)(2,1)S(1)}, bf16[1024,512]{0,1:T(8,128)(2,1)}, u32[]{:S(2)}) copy-start(bf16[1024,512]{0,1:T(8,128)(2,1)} %copy-done.8) | copy-start | bytes 3145732
  120.5 5.1 %copy-start.53 = (f32[1024,512]{1,0:T(8,128)S(1)}, f32[1024,512]{1,0:T(8,128)}, u32[]{:S(2)}) copy-start(f32[1024,512]{1,0:T(8,128)} %copy-done.51) | copy-start | bytes 6291460
  130.9 279.0 %all-reduce.5.cloned.1.call-start = ((), (), s32[]{:S(2)}) async-start(), calls=%async_computation.3 | async-start | bytes 3145728 | tf_op jit(solution)/shard_map/psum | solution.py:230
  140.1 4.7 %copy-start.14 = (bf16[1664,512]{1,0:T(8,128)(2,1)}, bf16[1664,512]{1,0:T(8,128)(2,1)S(1)}, u32[]{:S(2)}) copy-start(bf16[1664,512]{1,0:T(8,128)(2,1)S(1)} %get-tuple-element.56) | copy-start | bytes 5111812
  140.2 13.8 %collective-permute-start.12 = (bf16[256,512]{1,0:T(8,128)(2,1)S(1)}, bf16[256,512]{1,0:T(8,128)(2,1)S(1)}, u32[]{:S(2)}, u32[]{:S(2)}) collective-permute-start(bf16[256,512]{1,0:T(8,128)(2,1)S(1)} %get-tuple-element.25), channel_id=1, source_target_pairs={{0,7},{1,0},{2,1},{3,2},{4,3},{5,4},{6,5},{7,6},{8,15},{9,8},{10,9... | collective-permute-start | bytes 786440 | tf_op jit(solution)/shard_map/ppermute | solution.py:12
  141.6 12.4 %collective-permute-start.15 = (bf16[256,512]{1,0:T(8,128)(2,1)S(1)}, bf16[256,512]{1,0:T(8,128)(2,1)S(1)}, u32[]{:S(2)}, u32[]{:S(2)}) collective-permute-start(bf16[256,512]{1,0:T(8,128)(2,1)S(1)} %get-tuple-element.26), channel_id=1, source_target_pairs={{0,8},{8,16},{16,24},{24,0},{1,9},{9,17},{17,25},{25,1},{2,10},{10... | collective-permute-start | bytes 786440 | tf_op jit(solution)/shard_map/ppermute | solution.py:12
  141.6 12.4 %collective-permute-start.14 = (bf16[256,512]{1,0:T(8,128)(2,1)S(1)}, bf16[256,512]{1,0:T(8,128)(2,1)S(1)}, u32[]{:S(2)}, u32[]{:S(2)}) collective-permute-start(bf16[256,512]{1,0:T(8,128)(2,1)S(1)} %get-tuple-element.27), channel_id=1, source_target_pairs={{0,24},{8,0},{16,8},{24,16},{1,25},{9,1},{17,9},{25,17},{2,26},{10... | collective-permute-start | bytes 786440 | tf_op jit(solution)/shard_map/ppermute | solution.py:12
  143.4 16.1 %copy-start.30 = (s32[1,2,4,128]{3,1,2,0:T(2,128)S(1)}, s32[1,2,4,128]{3,1,2,0:T(2,128)}, u32[]{:S(2)}) copy-start(s32[1,2,4,128]{3,1,2,0:T(2,128)} %copy-done.29) | copy-start | bytes 12292
  143.4 16.1 %collective-permute-start.13 = (bf16[256,512]{1,0:T(8,128)(2,1)S(1)}, bf16[256,512]{1,0:T(8,128)(2,1)S(1)}, u32[]{:S(2)}, u32[]{:S(2)}) collective-permute-start(bf16[256,512]{1,0:T(8,128)(2,1)S(1)} %get-tuple-element.28), channel_id=1, source_target_pairs={{0,1},{1,2},{2,3},{3,4},{4,5},{5,6},{6,7},{7,0},{8,9},{9,10},{10,1... | collective-permute-start | bytes 786440 | tf_op jit(solution)/shard_map/ppermute | solution.py:12
  162.2 110.5 %copy-start.3 = (bf16[1024,512]{0,1:T(8,128)(2,1)S(1)}, bf16[1024,512]{0,1:T(8,128)(2,1)}, u32[]{:S(2)}) copy-start(bf16[1024,512]{0,1:T(8,128)(2,1)} %copy.32) | copy-start | bytes 3145732
  274.8 135.1 %copy-start.45 = (f32[10]{0:T(128)S(1)}, f32[10]{0:T(128)}, u32[]{:S(2)}) copy-start(f32[10]{0:T(128)} %constant.34.clone) | copy-start | bytes 124
  416.4 8.0 %copy-start.1 = (bf16[1024,512]{1,0:T(8,128)(2,1)S(1)}, bf16[1024,512]{1,0:T(8,128)(2,1)}, u32[]{:S(2)}) copy-start(bf16[1024,512]{1,0:T(8,128)(2,1)} %param.16) | copy-start | bytes 3145732
  (29 other events, 82.7 us)
Sparse Core Ops, SparseCore 0:
  131.1 141.5 all-reduce.2
  278.0 131.9 all-reduce.4
where the time goes:
time: 433 us; the launch traced here: 431 us
  waiting for transfers between devices  266 us (61%)
  matrix products  75.1 us (17%)
  starting transfers between devices  33.9 us (8%)
  local copies, waits for them, and re-layouts  26.5 us (6%)
  between operations  14.9 us (3%)
  other arithmetic  14.6 us (3%)
    psum x1, waiting for transfers between devices, on_device(): encode_grads = lax.psum(encode_grads, ('face', 'sub'))  129 us
    psum x1, waiting for transfers between devices, on_device(): process_grads = lax.psum(process_grads, ('face', 'sub'))  109 us
    dot_general x16, matrix products, product(): return jnp.dot(former, latter, preferred_element_type=jnp.float32)  33.8 us
    ppermute x16, waiting for transfers between devices, shifted(): return lax.ppermute(value, axis, pairs)  27.7 us
    ppermute x16, starting transfers between devices, shifted(): return lax.ppermute(value, axis, pairs)  26.2 us
    dot_general x16, matrix products, outer_sum(): lax.dot_general(former, latter, (((0,), (0,)), ((), ())), preferred_eleme...  26 us
    unnamed x132, local copies, waits for them, and re-layouts  20 us
    dot_general x8, matrix products, back_product(): lax.dot_general(former, latter, (((1,), (1,)), ((), ())), preferred_eleme...  15.3 us
  transfers between devices with their start and end apart: 20, of which 7 were waited for; matrix products, arithmetic and copies ran while one was open for 9% of the time, Pallas kernels for 0%

commit v1 on v0

--- a/solution.py
+++ b/solution.py
@@ -2,6 +2,7 @@
 import jax.numpy as jnp
 from jax import lax
 from jax.sharding import PartitionSpec as P
+from jax.lax import all_gather
 
 norm_eps = 1e-05
 
@@ -227,7 +228,8 @@
     grid_grad = back_product(cot_grid, weights[0]).astype(jnp.bfloat16)
     encode_grads = stack_grads([grad_encode_sender, grad_encode_receiver, grad_encode_output])
     encode_grads, process_grads = lax.optimization_barrier((encode_grads, process_grads))
-    encode_grads = lax.psum(encode_grads, ("face", "sub"))
+    _note_zone = lambda lane_axis, field_in: jnp.sum(all_gather(field_in, lane_axis), axis=0)
+    encode_grads = _note_zone(("face", "sub"), encode_grads)
     summed = jnp.concatenate([encode_grads, process_grads], axis=0).astype(jnp.float32)
     scale_column = jnp.array(
         [encode_scale] * 3 + [process_scale] * 4 + [update_scale] * 3, jnp.float32

time: 433 us -> 590 us (1.36)
  waiting for transfers between devices: 266 us -> 405 us
  other arithmetic: 14.6 us -> 29.3 us
    all_gather x0 -> x1, waiting for transfers between devices: none -> 268 us  [on_device(): all_gather(field_in, lane_axis)]
    psum x1 -> x0, waiting for transfers between devices: 129 us -> none  [on_device(): encode_grads = lax.psum(encode_grads, ('face', 'sub'))]
    reduce_sum x0 -> x1, other arithmetic: none -> 16.4 us  [on_device(): jnp.sum(all_gather(field_in, lane_axis), axis=0)]
    unnamed x132 -> x136, local copies, waits for them, and re-layouts: 20 us -> 20.8 us
  transfers between devices with their start and end apart: 20 -> 20, of which waited for: 7 -> 7; matrix products, arithmetic and copies ran while one was open for 9% -> 6% of each run, Pallas kernels for 0% -> 0%
where the time goes in v1:
time: 590 us; the launch traced here: 588 us
  waiting for transfers between devices  405 us (69%)
  matrix products  76.1 us (13%)
  starting transfers between devices  33.9 us (6%)
  local copies, waits for them, and re-layouts  29.6 us (5%)
  other arithmetic  29.3 us (5%)
  between operations  15 us (3%)
    all_gather x1, waiting for transfers between devices, on_device(): all_gather(field_in, lane_axis)  268 us
    psum x1, waiting for transfers between devices, on_device(): process_grads = lax.psum(process_grads, ('face', 'sub'))  109 us
    dot_general x16, matrix products, product(): return jnp.dot(former, latter, preferred_element_type=jnp.float32)  33.8 us
    dot_general x16, matrix products, outer_sum(): lax.dot_general(former, latter, (((0,), (0,)), ((), ())), preferred_eleme...  26.9 us
    ppermute x16, waiting for transfers between devices, shifted(): return lax.ppermute(value, axis, pairs)  26.8 us
    ppermute x16, starting transfers between devices, shifted(): return lax.ppermute(value, axis, pairs)  26.2 us
    unnamed x136, local copies, waits for them, and re-layouts  20.8 us
    reduce_sum x1, other arithmetic, on_device(): jnp.sum(all_gather(field_in, lane_axis), axis=0)  16.4 us
  transfers between devices with their start and end apart: 20, of which 7 were waited for; matrix products, arithmetic and copies ran while one was open for 6% of the time, Pallas kernels for 0%

profile of v1, /device:TPU:0, one launch (start us, length us, event | category | flops | bytes accessed | tf_op | source)
XLA Modules:
  0.0 588.4 jit_solution(15938592925978682079)
XLA Ops:
  8.0 2.4 constant_dynamic-update-slice_fusion.4
  12.2 2.5 collective-permute-start.3
  14.6 4.6 collective-permute-start.1
  19.2 3.1 fusion.81
  24.0 6.8 %collective-permute-done = bf16[256,512]{1,0:T(8,128)(2,1)S(1)} collective-permute-done((bf16[256,512]{1,0:T(8,128)(2,1)}, bf16[256,512]{1,0:T(8,128)(2,1)S(1)}, u32[]{:S(2)}, u32[]{:S(2)}) %collective-permute-start) | collective-permute-done | bytes 262176 | tf_op jit(solution)/shard_map/ppermute | solution.py:13
  33.7 1.9 fusion.50
  35.6 3.6 fusion.3
  39.2 2.3 fusion.146
  42.6 1.9 constant_dynamic-update-slice_fusion.10
  48.5 1.6 reshape.127
  50.1 5.0 all-to-all-start
  55.1 1.5 collective-permute-start.7
  56.6 4.3 collective-permute-start.5
  60.9 1.5 constant_dynamic-update-slice_fusion.9
  65.3 1.6 reshape.128
  66.8 1.6 constant_dynamic-update-slice_fusion.5
  68.4 1.9 fusion.49
  70.3 3.0 fusion.17
  73.3 2.3 fusion.147
  82.4 2.1 convolution_add_fusion.4
  84.5 4.3 fusion.141
  88.9 2.9 multiply_convert_fusion.4
  91.9 2.7 multiply_convert_fusion.3
  94.6 2.6 fusion.151
  97.2 1.5 fusion.30
  98.7 5.1 collective-permute-start.8
  106.0 2.6 all-to-all-start.1
  108.7 1.6 collective-permute-start.10
  110.4 1.7 collective-permute-start.9
  112.0 5.6 collective-permute-done.9
  120.5 1.9 fusion.140
  123.6 2.0 fusion.38
  125.7 1.6 fusion.33
  131.0 2.1 multiply_convert_fusion.2
  133.2 6.9 %fusion.152 = (bf16[1664,512]{1,0:T(8,128)(2,1)S(1)}, f32[1664,512]{1,0:T(8,128)}) fusion(f32[1024,512]{1,0:T(8,128)} %copy-done.57, bf16[1024,512]{0,1:T(8,128)(2,1)S(1)} %multiply_convert_fusion.2, bf16[10,512,512]{2,1,0:T(8,128)(2,1)} %param.26, s32[1024]{0:T(1024)S(1)} %copy-done.32, s32[1024]{0:T(1024)S(1)} %copy-done.50), kind=kOutput, calls=%fused_computation.225 | convolution fusion | flops 2292383744 | bytes 8790016 | tf_op jit(solution)/shard_map/dot_general | solution.py:43
  141.6 1.7 collective-permute-start.14
  146.1 7.9 %collective-permute-done.12 = bf16[256,512]{1,0:T(8,128)(2,1)S(1)} collective-permute-done((bf16[256,512]{1,0:T(8,128)(2,1)S(1)}, bf16[256,512]{1,0:T(8,128)(2,1)S(1)}, u32[]{:S(2)}, u32[]{:S(2)}) %collective-permute-start.12) | collective-permute-done | bytes 262176 | tf_op jit(solution)/shard_map/ppermute | solution.py:13
  154.0 5.5 collective-permute-done.13
  159.5 2.3 fusion.28
  163.2 109.5 %all-reduce.2.cloned.1.call-done = bf16[7,512,512]{1,2,0:T(8,128)(2,1)} async-done(((bf16[7,512,512]{1,2,0:T(8,128)(2,1)}), bf16[7,512,512]{1,2,0:T(8,128)(2,1)}) %all-reduce.2.cloned.1.call-update) | async-done | bytes 3670032 | tf_op jit(solution)/shard_map/psum | solution.py:215
  272.7 1.6 copy.66
  274.3 2.1 fusion.10
  277.7 2.1 fusion.48
  279.8 2.3 convolution_convert_fusion.1
  282.1 268.3 %all-gather.3.cloned.1.call-done = bf16[96,512,512]{2,1,0:T(8,128)(2,1)} async-done(((bf16[3,512,512]{2,1,0:T(8,128)(2,1)}), bf16[96,512,512]{2,1,0:T(8,128)(2,1)}) %all-gather.3.cloned.1.call-update) | async-done | bytes 50331664 | tf_op jit(solution)/shard_map/all_gather | solution.py:231
  550.4 16.4 %reduce_sum.156 = bf16[3,512,512]{2,1,0:T(8,128)(2,1)S(1)} reduce(bf16[32,3,512,512]{3,2,1,0:T(8,128)(2,1)} %bitcast.143, bf16[]{:T(256)} %constant.35.clone.1), dimensions={0}, to_apply=%region_13.14 | reduce | flops 24379392 | bytes 51904512 | tf_op jit(solution)/shard_map/reduce_sum | solution.py:231
  567.5 6.0 %multiply_convert_fusion = bf16[10,512,512]{1,2,0:T(8,128)(2,1)} fusion(bf16[7,512,512]{1,2,0:T(8,128)(2,1)} %all-reduce.2.cloned.1.call-done, bf16[3,512,512]{1,2,0:T(8,128)(2,1)S(1)} %copy.67, f32[10]{0:T(128)S(1)} %copy-done.45), kind=kLoop, calls=%fused_computation | loop fusion | flops 10485760 | bytes 10485800 | tf_op jit(solution)/shard_map/convert_element_type | solution.py:237
  573.6 8.0 %copy.69 = bf16[10,512,512]{2,1,0:T(8,128)(2,1)} copy(bf16[10,512,512]{1,2,0:T(8,128)(2,1)} %multiply_convert_fusion) | data formatting | bytes 10485760
  (208 shorter events, 39.2 us)
Async XLA Ops:
  7.2 12.0 %copy-start = (bf16[1024,512]{1,0:T(8,128)(2,1)S(1)}, bf16[1024,512]{1,0:T(8,128)(2,1)}, u32[]{:S(2)}) copy-start(bf16[1024,512]{1,0:T(8,128)(2,1)} %param.16) | copy-start | bytes 3145732
  10.4 8.8 %copy-start.25 = (s32[1024]{0:T(1024)S(1)}, s32[1024]{0:T(1024)}, u32[]{:S(2)}) copy-start(s32[1024]{0:T(1024)} %param.21) | copy-start | bytes 12292
  12.2 10.1 %copy-start.22 = (s32[1024]{0:T(1024)S(1)}, s32[1024]{0:T(1024)}, u32[]{:S(2)}) copy-start(s32[1024]{0:T(1024)} %param.25) | copy-start | bytes 12292
  12.2 10.1 %copy-start.38 = (s32[1,4,64]{2,1,0:T(4,128)S(1)}, s32[1,4,64]{2,1,0:T(4,128)}, u32[]{:S(2)}) copy-start(s32[1,4,64]{2,1,0:T(4,128)} %param.22) | copy-start | bytes 3076
  12.2 10.2 %copy-start.37 = (s32[1,32,4]{1,2,0:T(4,128)S(1)}, s32[1,32,4]{1,2,0:T(4,128)}, u32[]{:S(2)}) copy-start(s32[1,32,4]{1,2,0:T(4,128)} %param.23) | copy-start | bytes 1540
  12.2 10.4 %copy-start.10 = (bf16[1024,512]{1,0:T(8,128)(2,1)S(1)}, bf16[1024,512]{1,0:T(8,128)(2,1)}, u32[]{:S(2)}) copy-start(bf16[1024,512]{1,0:T(8,128)(2,1)} %param.18) | copy-start | bytes 3145732
  12.2 20.8 %collective-permute-start.3 = (bf16[256,512]{1,0:T(8,128)(2,1)}, bf16[256,512]{1,0:T(8,128)(2,1)S(1)}, u32[]{:S(2)}, u32[]{:S(2)}) collective-permute-start(bf16[256,512]{1,0:T(8,128)(2,1)} %get-tuple-element.39), channel_id=1, source_target_pairs={{0,24},{8,0},{16,8},{24,16},{1,25},{9,1},{17,9},{25,17},{2,26},{10... | collective-permute-start | bytes 786440 | tf_op jit(solution)/shard_map/ppermute | solution.py:13
  14.6 17.6 %collective-permute-start.2 = (bf16[256,512]{1,0:T(8,128)(2,1)}, bf16[256,512]{1,0:T(8,128)(2,1)S(1)}, u32[]{:S(2)}, u32[]{:S(2)}) collective-permute-start(bf16[256,512]{1,0:T(8,128)(2,1)} %get-tuple-element.40), channel_id=1, source_target_pairs={{0,8},{8,16},{16,24},{24,0},{1,9},{9,17},{17,25},{25,1},{2,10},{10... | collective-permute-start | bytes 786440 | tf_op jit(solution)/shard_map/ppermute | solution.py:13
  14.6 16.9 %collective-permute-start.1 = (bf16[256,512]{1,0:T(8,128)(2,1)}, bf16[256,512]{1,0:T(8,128)(2,1)S(1)}, u32[]{:S(2)}, u32[]{:S(2)}) collective-permute-start(bf16[256,512]{1,0:T(8,128)(2,1)} %get-tuple-element.41), channel_id=1, source_target_pairs={{0,7},{1,0},{2,1},{3,2},{4,3},{5,4},{6,5},{7,6},{8,15},{9,8},{10,9... | collective-permute-start | bytes 786440 | tf_op jit(solution)/shard_map/ppermute | solution.py:13
  19.2 11.6 %collective-permute-start = (bf16[256,512]{1,0:T(8,128)(2,1)}, bf16[256,512]{1,0:T(8,128)(2,1)S(1)}, u32[]{:S(2)}, u32[]{:S(2)}) collective-permute-start(bf16[256,512]{1,0:T(8,128)(2,1)} %get-tuple-element.42), channel_id=1, source_target_pairs={{0,1},{1,2},{2,3},{3,4},{4,5},{5,6},{6,7},{7,0},{8,9},{9,10},{10,1... | collective-permute-start | bytes 786440 | tf_op jit(solution)/shard_map/ppermute | solution.py:13
  19.2 16.4 %copy-start.31 = (s32[1024]{0:T(1024)}, s32[1024]{0:T(1024)S(1)}, u32[]{:S(2)}) copy-start(s32[1024]{0:T(1024)S(1)} %broadcast_add_fusion.1) | copy-start | bytes 12292
  22.3 48.0 %copy-start.33 = (s32[1024]{0:T(1024)}, s32[1024]{0:T(1024)S(1)}, u32[]{:S(2)}) copy-start(s32[1024]{0:T(1024)S(1)} %broadcast_add_fusion) | copy-start | bytes 12292
  22.6 21.9 %copy-start.27 = (s32[384]{0:T(512)}, s32[384]{0:T(512)S(1)}, u32[]{:S(2)}) copy-start(s32[384]{0:T(512)S(1)} %pad_add_fusion) | copy-start | bytes 4612
  22.6 11.1 %copy-start.16 = (bf16[128,512]{1,0:T(8,128)(2,1)S(1)}, bf16[128,512]{1,0:T(8,128)(2,1)}, u32[]{:S(2)}) copy-start(bf16[128,512]{1,0:T(8,128)(2,1)} %param.15) | copy-start | bytes 393220
  22.6 13.0 %copy-start.49 = (s32[1024]{0:T(1024)S(1)}, s32[1024]{0:T(1024)}, u32[]{:S(2)}) copy-start(s32[1024]{0:T(1024)} %param.20) | copy-start | bytes 12292
  44.8 25.5 %copy-start.47 = (s32[1024]{0:T(1024)S(1)}, s32[1024]{0:T(1024)}, u32[]{:S(2)}) copy-start(s32[1024]{0:T(1024)} %param.24) | copy-start | bytes 12292
  45.5 15.3 %collective-permute-start.4 = (bf16[64,512]{1,0:T(8,128)(2,1)}, bf16[64,512]{1,0:T(8,128)(2,1)}, u32[]{:S(2)}, u32[]{:S(2)}) collective-permute-start(bf16[64,512]{1,0:T(8,128)(2,1)} %get-tuple-element.50), channel_id=1, source_target_pairs={{0,1},{1,2},{2,3},{3,4},{4,5},{5,6},{6,7},{7,0},{8,9},{9,10},{10,1... | collective-permute-start | bytes 196616 | tf_op jit(solution)/shard_map/ppermute | solution.py:13
  50.1 15.1 %all-to-all-start = ((bf16[32,4,512]{2,1,0:T(4,128)(2,1)}), bf16[32,4,512]{2,1,0:T(4,128)(2,1)}, u32[]{:S(2)}, u32[]{:S(2)}) async-start(bf16[32,4,512]{2,1,0:T(4,128)(2,1)} %reshape.127), calls=%async_computation | async-start | bytes 262144 | tf_op jit(solution)/shard_map/all_to_all | solution.py:94
  55.1 9.5 %collective-permute-start.7 = (bf16[64,512]{1,0:T(8,128)(2,1)}, bf16[64,512]{1,0:T(8,128)(2,1)S(1)}, u32[]{:S(2)}, u32[]{:S(2)}) collective-permute-start(bf16[64,512]{1,0:T(8,128)(2,1)} %get-tuple-element.47), channel_id=1, source_target_pairs={{0,24},{8,0},{16,8},{24,16},{1,25},{9,1},{17,9},{25,17},{2,26},{10... | collective-permute-start | bytes 196616 | tf_op jit(solution)/shard_map/ppermute | solution.py:13
  56.6 7.4 %collective-permute-start.6 = (bf16[64,512]{1,0:T(8,128)(2,1)}, bf16[64,512]{1,0:T(8,128)(2,1)S(1)}, u32[]{:S(2)}, u32[]{:S(2)}) collective-permute-start(bf16[64,512]{1,0:T(8,128)(2,1)} %get-tuple-element.48), channel_id=1, source_target_pairs={{0,8},{8,16},{16,24},{24,0},{1,9},{9,17},{17,25},{25,1},{2,10},{10... | collective-permute-start | bytes 196616 | tf_op jit(solution)/shard_map/ppermute | solution.py:13
  56.6 6.8 %collective-permute-start.5 = (bf16[64,512]{1,0:T(8,128)(2,1)}, bf16[64,512]{1,0:T(8,128)(2,1)S(1)}, u32[]{:S(2)}, u32[]{:S(2)}) collective-permute-start(bf16[64,512]{1,0:T(8,128)(2,1)} %get-tuple-element.49), channel_id=1, source_target_pairs={{0,7},{1,0},{2,1},{3,2},{4,3},{5,4},{6,5},{7,6},{8,15},{9,8},{10,9... | collective-permute-start | bytes 196616 | tf_op jit(solution)/shard_map/ppermute | solution.py:13
  77.1 5.3 copy-start.6
  80.2 4.3 copy-start.39
  80.2 4.3 copy-start.24
  81.0 7.9 %copy-start.41 = (f32[128]{0:T(128)}, f32[128]{0:T(128)S(1)}, u32[]{:S(2)}) copy-start(f32[128]{0:T(128)S(1)} %get-tuple-element.68) | copy-start | bytes 1540
  81.0 7.9 %copy-start.43 = (f32[128]{0:T(128)}, f32[128]{0:T(128)S(1)}, u32[]{:S(2)}) copy-start(f32[128]{0:T(128)S(1)} %get-tuple-element.69) | copy-start | bytes 1540
  82.4 6.5 %copy-start.4 = (bf16[128,512]{1,0:T(8,128)(2,1)}, bf16[128,512]{1,0:T(8,128)(2,1)S(1)}, u32[]{:S(2)}) copy-start(bf16[128,512]{1,0:T(8,128)(2,1)S(1)} %fusion.46) | copy-start | bytes 393220
  97.2 8.1 %copy-start.15 = (bf16[640,512]{1,0:T(8,128)(2,1)}, bf16[640,512]{1,0:T(8,128)(2,1)S(1)}, u32[]{:S(2)}) copy-start(bf16[640,512]{1,0:T(8,128)(2,1)S(1)} %get-tuple-element.63) | copy-start | bytes 1966084
  97.2 6.7 %copy-start.13 = (f32[128,512]{1,0:T(8,128)S(1)}, f32[128,512]{1,0:T(8,128)}, u32[]{:S(2)}) copy-start(f32[128,512]{1,0:T(8,128)} %convolution_add_fusion.4) | copy-start | bytes 786436
  98.7 19.1 %copy-start.28 = (s32[384]{0:T(512)S(1)}, s32[384]{0:T(512)}, u32[]{:S(2)}) copy-start(s32[384]{0:T(512)} %copy-done.27) | copy-start | bytes 4612
  98.7 13.3 %collective-permute-start.8 = (bf16[64,512]{1,0:T(8,128)(2,1)S(1)}, bf16[64,512]{1,0:T(8,128)(2,1)S(1)}, u32[]{:S(2)}, u32[]{:S(2)}) collective-permute-start(bf16[64,512]{1,0:T(8,128)(2,1)S(1)} %get-tuple-element.46), channel_id=1, source_target_pairs={{0,7},{1,0},{2,1},{3,2},{4,3},{5,4},{6,5},{7,6},{8,15},{9,8},{10,9... | collective-permute-start | bytes 196616 | tf_op jit(solution)/shard_map/ppermute | solution.py:13
  105.2 15.2 %copy-start.26 = (s32[1024]{0:T(1024)S(1)}, s32[1024]{0:T(1024)}, u32[]{:S(2)}) copy-start(s32[1024]{0:T(1024)} %param.21) | copy-start | bytes 12292
  106.0 11.8 %all-to-all-start.1 = ((bf16[32,4,512]{2,1,0:T(4,128)(2,1)}), bf16[32,4,512]{2,1,0:T(4,128)(2,1)S(1)}, u32[]{:S(2)}, u32[]{:S(2)}) async-start(bf16[32,4,512]{2,1,0:T(4,128)(2,1)} %reshape.129), calls=%async_computation.1 | async-start | bytes 262144 | tf_op jit(solution)/shard_map/all_to_all | solution.py:98
  108.5 164.1 %all-reduce.2.cloned.1.call-start = ((), (), s32[]{:S(2)}) async-start(), calls=%async_computation.2 | async-start | bytes 7340032 | tf_op jit(solution)/shard_map/psum | solution.py:215
  108.6 9.1 %collective-permute-start.11 = (bf16[64,512]{1,0:T(8,128)(2,1)S(1)}, bf16[64,512]{1,0:T(8,128)(2,1)S(1)}, u32[]{:S(2)}, u32[]{:S(2)}) collective-permute-start(bf16[64,512]{1,0:T(8,128)(2,1)S(1)} %get-tuple-element.43), channel_id=1, source_target_pairs={{0,8},{8,16},{16,24},{24,0},{1,9},{9,17},{17,25},{25,1},{2,10},{10... | collective-permute-start | bytes 196616 | tf_op jit(solution)/shard_map/ppermute | solution.py:13
  108.7 8.9 %collective-permute-start.10 = (bf16[64,512]{1,0:T(8,128)(2,1)S(1)}, bf16[64,512]{1,0:T(8,128)(2,1)S(1)}, u32[]{:S(2)}, u32[]{:S(2)}) collective-permute-start(bf16[64,512]{1,0:T(8,128)(2,1)S(1)} %get-tuple-element.44), channel_id=1, source_target_pairs={{0,24},{8,0},{16,8},{24,16},{1,25},{9,1},{17,9},{25,17},{2,26},{10... | collective-permute-start | bytes 196616 | tf_op jit(solution)/shard_map/ppermute | solution.py:13
  110.4 7.3 %collective-permute-start.9 = (bf16[64,512]{1,0:T(8,128)(2,1)S(1)}, bf16[64,512]{1,0:T(8,128)(2,1)S(1)}, u32[]{:S(2)}, u32[]{:S(2)}) collective-permute-start(bf16[64,512]{1,0:T(8,128)(2,1)S(1)} %get-tuple-element.45), channel_id=1, source_target_pairs={{0,1},{1,2},{2,3},{3,4},{4,5},{5,6},{6,7},{7,0},{8,9},{9,10},{10,1... | collective-permute-start | bytes 196616 | tf_op jit(solution)/shard_map/ppermute | solution.py:13
  120.5 5.1 copy-start.9
  120.5 5.1 copy-start.55
  125.6 4.0 copy-start.12
  130.9 419.5 %all-gather.3.cloned.1.call-start = ((), (), s32[]{:S(2)}) async-start(), calls=%async_computation.3 | async-start | bytes 51904512 | tf_op jit(solution)/shard_map/all_gather | solution.py:231
  140.2 13.8 %collective-permute-start.12 = (bf16[256,512]{1,0:T(8,128)(2,1)S(1)}, bf16[256,512]{1,0:T(8,128)(2,1)S(1)}, u32[]{:S(2)}, u32[]{:S(2)}) collective-permute-start(bf16[256,512]{1,0:T(8,128)(2,1)S(1)} %get-tuple-element.35), channel_id=1, source_target_pairs={{0,7},{1,0},{2,1},{3,2},{4,3},{5,4},{6,5},{7,6},{8,15},{9,8},{10,9... | collective-permute-start | bytes 786440 | tf_op jit(solution)/shard_map/ppermute | solution.py:13
  141.6 12.3 %collective-permute-start.15 = (bf16[256,512]{1,0:T(8,128)(2,1)S(1)}, bf16[256,512]{1,0:T(8,128)(2,1)S(1)}, u32[]{:S(2)}, u32[]{:S(2)}) collective-permute-start(bf16[256,512]{1,0:T(8,128)(2,1)S(1)} %get-tuple-element.36), channel_id=1, source_target_pairs={{0,8},{8,16},{16,24},{24,0},{1,9},{9,17},{17,25},{25,1},{2,10},{10... | collective-permute-start | bytes 786440 | tf_op jit(solution)/shard_map/ppermute | solution.py:13
  141.6 12.3 %collective-permute-start.14 = (bf16[256,512]{1,0:T(8,128)(2,1)S(1)}, bf16[256,512]{1,0:T(8,128)(2,1)S(1)}, u32[]{:S(2)}, u32[]{:S(2)}) collective-permute-start(bf16[256,512]{1,0:T(8,128)(2,1)S(1)} %get-tuple-element.37), channel_id=1, source_target_pairs={{0,24},{8,0},{16,8},{24,16},{1,25},{9,1},{17,9},{25,17},{2,26},{10... | collective-permute-start | bytes 786440 | tf_op jit(solution)/shard_map/ppermute | solution.py:13
  143.4 16.1 %copy-start.30 = (s32[1,2,4,128]{3,1,2,0:T(2,128)S(1)}, s32[1,2,4,128]{3,1,2,0:T(2,128)}, u32[]{:S(2)}) copy-start(s32[1,2,4,128]{3,1,2,0:T(2,128)} %copy-done.29) | copy-start | bytes 12292
  143.4 16.1 %collective-permute-start.13 = (bf16[256,512]{1,0:T(8,128)(2,1)S(1)}, bf16[256,512]{1,0:T(8,128)(2,1)S(1)}, u32[]{:S(2)}, u32[]{:S(2)}) collective-permute-start(bf16[256,512]{1,0:T(8,128)(2,1)S(1)} %get-tuple-element.38), channel_id=1, source_target_pairs={{0,1},{1,2},{2,3},{3,4},{4,5},{5,6},{6,7},{7,0},{8,9},{9,10},{10,1... | collective-permute-start | bytes 786440 | tf_op jit(solution)/shard_map/ppermute | solution.py:13
  163.2 111.1 %copy-start.3 = (bf16[1024,512]{0,1:T(8,128)(2,1)S(1)}, bf16[1024,512]{0,1:T(8,128)(2,1)}, u32[]{:S(2)}) copy-start(bf16[1024,512]{0,1:T(8,128)(2,1)} %copy.57) | copy-start | bytes 3145732
  573.6 8.0 %copy-start.1 = (bf16[1024,512]{1,0:T(8,128)(2,1)S(1)}, bf16[1024,512]{1,0:T(8,128)(2,1)}, u32[]{:S(2)}) copy-start(bf16[1024,512]{1,0:T(8,128)(2,1)} %param.16) | copy-start | bytes 3145732
  (31 other events, 84.1 us)
Sparse Core Ops, SparseCore 0:
  131.0 141.5 all-reduce.1
  276.2 274.2 all-gather.2
